TPU v7x, 32 devices: a whole 2x2x4 slice. The times are simulated.
32 devices in a mesh: dp: 8 (over z, x), mp: 4 (over y, core).
Axes of the slice: x: 2, y: 2, z: 4, core: 2. Of those that a mesh axis runs over, the one named last changes fastest.
Arguments:
- sparse_vecs: bfloat16 [8192, 26, 128], P(('dp', 'mp')), may hold values from -6 to 6
- dense_vec: bfloat16 [8192, 128], P(('dp', 'mp')), may hold values from -6 to 6
- top_cot: bfloat16 [8192, 1024], P(('dp', 'mp')), may hold values from -0.59765625 to 0.59765625
- top_weight: bfloat16 [479, 1024], replicated, may hold values from -0.25 to 0.25
- owner_ids: int32 [8192, 26, 1], P(('dp', 'mp')), may hold values from 0 to 7; in each aligned block of 6656 rows (0 to 6655, 6656 to 13311, ..., all dimensions but the last counted through in order) at most 1664 rows name the same one
- local_rows: int32 [8192, 26], P(('dp', 'mp')), may hold values from 0 to 127
- table: float32 [26, 1024, 128], P(None, ('dp', 'mp')), may hold values from -0.6 to 0.6
- accum: float32 [26, 1024], P(None, ('dp', 'mp')), may hold values from 0.05 to 2
Outputs:
- dense_grad: bfloat16 [8192, 128], P(('dp', 'mp'))
- new_table: float32 [26, 1024, 128], P(None, ('dp', 'mp'))
- new_accum: float32 [26, 1024], P(None, ('dp', 'mp'))
Inputs may be any that keep to these rules, and one draw needn't show every extreme that they name: `owner_ids`: among the lookups of one device's 256 samples no owner group is named more than 1664 times; in every draw some device names some owner group exactly 1664 times.
All inputs are finite; a program needn't handle non-finite values.
Results may differ from a plain program's by a relative error of at most 0.005.
Values may be sent and summed in bfloat16 or wider, within the bound.
A program may use at most 128 MiB of HBM per device.

v0:
```python
import functools

import jax
import jax.numpy as jnp
import numpy as np
from jax import lax
from jax.experimental import pallas as pl
from jax.experimental.pallas import tpu as pltpu
from jax.sharding import PartitionSpec as P

LEARN_RATE = 0.1
EPSILON = 1e-08
MESH = pl.DeviceIdType.MESH
CHUNKS = 6
LEAD = 4
VMEM_LIMIT = 60 * 1024 * 1024


def pair_matrix(feature_count):
    row_index, col_index = np.tril_indices(feature_count, -1)
    pair_count = row_index.shape[0]
    matrix = np.zeros((pair_count, feature_count * feature_count), np.float32)
    matrix[np.arange(pair_count), row_index * feature_count + col_index] = 1.0
    matrix[np.arange(pair_count), col_index * feature_count + row_index] = 1.0
    return jnp.asarray(matrix)


def table_chunks(table_count):
    cut = (table_count + 1) // 2
    halves = []
    for half, (low, high) in enumerate(((0, cut), (cut, table_count))):
        edges = [low + (high - low) * k // CHUNKS for k in range(CHUNKS + 1)]
        halves.append([(half, a, b - a) for a, b in zip(edges, edges[1:]) if b > a])
    out = []
    for k in range(CHUNKS):
        for pieces in halves:
            if k < len(pieces):
                out.append(pieces[k])
    return cut, out


def neighbours():
    dp, mp = lax.axis_index("dp"), lax.axis_index("mp")
    mp_count = lax.axis_size("mp")
    across_x = (dp + 1 - 2 * (dp % 2), mp)
    across_y = (dp, (mp + mp_count // 2) % mp_count)
    core = (dp, mp + 1 - 2 * (mp % 2))
    return across_x, across_y, core


def meet(devices):
    barrier = pltpu.get_barrier_semaphore()
    for device in devices:
        pl.semaphore_signal(barrier, inc=1, device_id=device, device_id_type=MESH)
    pl.semaphore_wait(barrier, len(devices))


def route_kernel(
    chunks, z_count, rows, keys, out, got_rows, got_keys, partial, first, mixed, last,
    send, recv, send1, recv1, send2, recv2,
):
    across_x, across_y, core = neighbours()
    dp, mp = lax.axis_index("dp"), lax.axis_index("mp")
    z = dp // 2
    my_side = (mp // 2, dp % 2)
    rows_own = out.shape[1]
    side_rows = z_count * rows_own
    bases = (mp * 2 * side_rows, ((mp % 2) * 2 + dp % 2) * 2 * side_rows)
    z_devices = [(((z + d) % z_count) * 2 + dp % 2, mp) for d in range(1, z_count)]
    meet([across_x, across_y, core] + z_devices)
    count = len(chunks)

    def copies(leg, index, source_rows, source_keys, slot, device):
        _, start, length = chunks[index]
        span = pl.ds(start, length)
        return [
            pltpu.make_async_remote_copy(
                src_ref=source.at[span],
                dst_ref=target.at[slot, span],
                send_sem=send.at[leg, index, which],
                recv_sem=recv.at[leg, index, which],
                device_id=device,
                device_id_type=MESH,
            )
            for which, (source, target) in enumerate(
                ((source_rows, got_rows), (source_keys, got_keys))
            )
        ]

    started = []

    def begin(group):
        for copy in group:
            copy.start()
        started.extend(group)
        return group

    outward, inward, relayed, swaps, spread = [], [], [], [], []

    def send_out(index):
        if index < count:
            half = chunks[index][0]
            outward.append(
                begin(copies(1, index, rows, keys, 1, across_x if half else across_y))
            )
            inward.append(begin(copies(0, index, rows, keys, 0, core)))

    def relay(index):
        for copy in outward[index]:
            copy.wait_recv()
        relayed.append(begin(copies(2, index, got_rows.at[1], got_keys.at[1], 2, core)))

    def sums(index):
        half, start, length = chunks[index]
        for copy in inward[index] + relayed[index]:
            copy.wait_recv()
        base = bases[half]
        batch_rows = rows.shape[1]
        targets = lax.broadcasted_iota(jnp.int32, (2 * side_rows, batch_rows), 0)

        def add_table(step, carry):
            t = start + step

            def part(key_row, row_block):
                onehot = jnp.where(targets == key_row - base, 1.0, 0.0).astype(jnp.bfloat16)
                return jnp.dot(onehot, row_block, preferred_element_type=jnp.float32)

            total = part(keys[t], rows[t])
            for slot in range(3):
                total = total + part(got_keys[slot, t], got_rows[slot, t])
            total = total.astype(jnp.bfloat16)
            partial[t, 0] = total[:side_rows]
            partial[t, 1] = total[side_rows:]
            return carry

        lax.fori_loop(0, length, add_table, 0)
        span = pl.ds(start, length)
        other = 1 - (my_side[0] if half else my_side[1])
        swaps.append(
            pltpu.make_async_remote_copy(
                src_ref=partial.at[span, other],
                dst_ref=first.at[span],
                send_sem=send1.at[index],
                recv_sem=recv1.at[index],
                device_id=across_y if half else across_x,
                device_id_type=MESH,
            )
        )
        begin(swaps[-1:])

    def along_z(index):
        half, start, length = chunks[index]
        mine = my_side[0] if half else my_side[1]
        swaps[index].wait_recv()

        def add(step, carry):
            t = start + step
            total = partial[t, mine].astype(jnp.float32) + first[t].astype(jnp.float32)
            total = total.astype(jnp.bfloat16)
            for owner in range(z_count):
                mixed[owner, t] = total[owner * rows_own : (owner + 1) * rows_own]
            return carry

        lax.fori_loop(0, length, add, 0)
        span = pl.ds(start, length)
        group = [
            pltpu.make_async_remote_copy(
                src_ref=mixed.at[(z + d) % z_count, span],
                dst_ref=last.at[d - 1, span],
                send_sem=send2.at[index, d - 1],
                recv_sem=recv2.at[index, d - 1],
                device_id=z_devices[d - 1],
                device_id_type=MESH,
            )
            for d in range(1, z_count)
        ]
        spread.append(begin(group))

    def finish(index):
        _, start, length = chunks[index]
        for copy in spread[index]:
            copy.wait_recv()

        def add(step, carry):
            t = start + step
            total = mixed[z, t].astype(jnp.float32)
            for d in range(1, z_count):
                total = total + last[d - 1, t].astype(jnp.float32)
            out[t] = total
            return carry

        lax.fori_loop(0, length, add, 0)

    for index in range(LEAD):
        send_out(index)
    for index in range(count + 3):
        if index < count:
            relay(index)
            send_out(index + LEAD)
        if 0 <= index - 1 < count:
            sums(index - 1)
        if 0 <= index - 3 < count:
            along_z(index - 3)
    for index in range(count):
        finish(index)
    for copy in started:
        copy.wait_send()


def route(chunks, z_count, rows_own, rows, keys):
    table_count, batch_rows, width = rows.shape
    side_rows = z_count * rows_own
    others = max(1, z_count - 1)
    vmem = pl.BlockSpec(memory_space=pltpu.VMEM)
    count = len(chunks)
    return pl.pallas_call(
        functools.partial(route_kernel, chunks, z_count),
        out_shape=jax.ShapeDtypeStruct((table_count, rows_own, width), jnp.float32),
        in_specs=[vmem] * 2,
        out_specs=vmem,
        scratch_shapes=[
            pltpu.VMEM((3,) + rows.shape, rows.dtype),
            pltpu.VMEM((3,) + keys.shape, keys.dtype),
            pltpu.VMEM((table_count, 2, side_rows, width), jnp.bfloat16),
            pltpu.VMEM((table_count, side_rows, width), jnp.bfloat16),
            pltpu.VMEM((z_count, table_count, rows_own, width), jnp.bfloat16),
            pltpu.VMEM((others, table_count, rows_own, width), jnp.bfloat16),
            pltpu.SemaphoreType.DMA((3, count, 2)),
            pltpu.SemaphoreType.DMA((3, count, 2)),
            pltpu.SemaphoreType.DMA((count,)),
            pltpu.SemaphoreType.DMA((count,)),
            pltpu.SemaphoreType.DMA((count, others)),
            pltpu.SemaphoreType.DMA((count, others)),
        ],
        compiler_params=pltpu.CompilerParams(
            collective_id=0, has_side_effects=True, vmem_limit_bytes=VMEM_LIMIT
        ),
    )(rows, keys)


def encode_keys(cut, z_count, rows_own, owner, local):
    x, z = owner % 2, owner // 2
    mp, row = local // rows_own, local % rows_own
    y, core = mp // 2, mp % 2
    place = z * rows_own + row
    by_x = (mp * 2 + x) * (z_count * rows_own) + place
    by_y = ((core * 2 + x) * 2 + y) * (z_count * rows_own) + place
    first_half = jnp.arange(owner.shape[1])[None, :] < cut
    return jnp.where(first_half, by_x, by_y).T[:, None, :]


def per_device(sparse_vecs, dense_vec, top_cot, top_weight, owner_ids, local_rows, table, accum):
    batch_rows, table_count, row_width = sparse_vecs.shape
    feature_count = table_count + 1
    rows_own = table.shape[1]
    z_count = lax.axis_size("dp") // 2
    cut, chunks = table_chunks(table_count)
    keys = encode_keys(cut, z_count, rows_own, owner_ids[:, :, 0], local_rows)
    input_cot = jnp.einsum("bh,zh->bz", top_cot, top_weight, preferred_element_type=jnp.float32)
    symmetric = jnp.dot(
        input_cot[:, row_width:].astype(jnp.bfloat16),
        pair_matrix(feature_count).astype(jnp.bfloat16),
        preferred_element_type=jnp.bfloat16,
    )
    symmetric = symmetric.reshape(batch_rows, feature_count, feature_count)
    features = jnp.concatenate([dense_vec[:, None, :], sparse_vecs], axis=1)
    feature_grad = jnp.einsum(
        "bij,bje->bie", symmetric, features, preferred_element_type=jnp.float32
    )
    dense_grad = (input_cot[:, :row_width] + feature_grad[:, 0]).astype(jnp.bfloat16)
    rows = feature_grad[:, 1:].astype(jnp.bfloat16).transpose(1, 0, 2)
    row_grad = route(chunks, z_count, rows_own, rows, keys)
    new_accum = accum + jnp.mean(row_grad * row_grad, axis=-1)
    new_table = table - LEARN_RATE * row_grad / (jnp.sqrt(new_accum)[:, :, None] + EPSILON)
    return (dense_grad, new_table, new_accum)


def solution(mesh):
    in_specs = (
        P(("dp", "mp"), None, None),
        P(("dp", "mp"), None),
        P(("dp", "mp"), None),
        P(),
        P(("dp", "mp"), None, None),
        P(("dp", "mp"), None),
        P(None, ("dp", "mp"), None),
        P(None, ("dp", "mp")),
    )
    out_specs = (P(("dp", "mp"), None), P(None, ("dp", "mp"), None), P(None, ("dp", "mp")))
    return jax.shard_map(
        per_device, mesh=mesh, in_specs=in_specs, out_specs=out_specs, check_vma=False
    )
```

profile of v0, /device:TPU:0, one launch (start us, length us, event | category | flops | bytes accessed | tf_op | source)
XLA Modules:
  0.0 69.6 jit_solution(7841515104360677797)
XLA Ops:
  0.6 0.0 copy-start
  0.6 0.0 copy-start.3
  0.7 1.2 %copy-done = bf16[479,1024]{1,0:T(8,128)(2,1)S(1)} copy-done((bf16[479,1024]{1,0:T(8,128)(2,1)S(1)}, bf16[479,1024]{1,0:T(8,128)(2,1)}, u32[]{:S(2)}) %copy-start) | copy-done | bytes 981016
  1.8 1.5 %fusion.29 = f32[256,479]{0,1:T(8,128)S(1)} fusion(bf16[256,1024]{1,0:T(8,128)(2,1)} %param.11, bf16[479,1024]{1,0:T(8,128)(2,1)S(1)} %copy-done), kind=kOutput, calls=%fused_computation.56 | convolution fusion | flops 251133952 | bytes 1995776 | tf_op jit(solution)/shard_map/bh,zh->bz/dot_general | solution.py:259
  3.3 0.0 copy-start.2
  3.4 0.8 %copy-done.2 = f32[256,479]{0,1:T(8,128)} copy-done((f32[256,479]{0,1:T(8,128)}, f32[256,479]{0,1:T(8,128)S(1)}, u32[]{:S(2)}) %copy-start.2) | copy-done | bytes 490520
  4.1 0.0 copy-done.3
  4.1 0.4 fusion.5
  4.5 0.1 reshape.16
  4.7 3.2 %copy.19 = bf16[256,27,27]{2,1,0:T(8,128)(2,1)S(1)} copy(bf16[256,27,27]{0,2,1:T(8,128)(2,1)S(1)} %reshape.16) | data formatting | bytes 746496 | tf_op jit(solution)/shard_map/reshape | solution.py:265
  7.9 0.0 copy-start.5
  7.9 2.6 %copy.18 = bf16[256,26,128]{2,1,0:T(8,128)(2,1)S(1)} copy(bf16[256,26,128]{2,0,1:T(8,128)(2,1)} %param.9) | data formatting | bytes 3407872 | tf_op args[0]
  10.5 0.0 copy-done.5
  10.5 0.1 copy.17
  10.6 0.8 %fusion = f32[256,27,128]{2,1,0:T(8,128)S(1)} fusion(bf16[256,27,27]{2,1,0:T(8,128)(2,1)S(1)} %copy.19, bf16[256,26,128]{2,1,0:T(8,128)(2,1)S(1)} %copy.18, bf16[256,1,128]{2,1,0:T(2,128)(2,1)S(1)} %copy.17), kind=kOutput, calls=%fused_computation.1 | convolution fusion | flops 51314688 | bytes 5681664 | tf_op jit(solution)/shard_map/bij,bje->bie/dot_general | solution.py:267
  11.4 0.0 copy-start.1
  11.4 0.6 slice.21
  12.0 0.0 copy-start.6
  12.0 0.0 copy-start.7
  12.0 1.9 %copy.48 = bf16[256,26,128]{2,0,1:T(8,128)(2,1)} copy(bf16[256,26,128]{2,1,0:T(8,128)(2,1)S(1)} %slice.21) | data formatting | bytes 3407872
  14.0 0.0 copy-done.1
  14.0 0.0 copy-start.8
  14.0 0.0 copy-start.4
  14.0 0.0 copy-done.6
  14.0 0.0 copy-done.7
  14.0 0.1 fusion.16
  14.1 0.6 broadcast_in_dim.18.keys
  14.7 48.1 %shard_map.112 = f32[26,32,128]{2,1,0:T(8,128)} custom-call(bf16[26,256,128]{2,1,0:T(8,128)(2,1)} %bitcast.34, s32[26,1,256]{2,1,0:T(1,128)} %broadcast_in_dim.18.keys), custom_call_target="tpu_custom_call" | custom-call | tf_op jit(solution)/shard_map/pallas_call | solution.py:216
  62.8 1.2 %multiply_reduce_fusion = f32[26,32]{1,0:T(8,128)S(1)} fusion(f32[26,32,128]{2,1,0:T(8,128)} %shard_map.112), kind=kLoop, calls=%fused_computation.7 | loop fusion | flops 212160 | bytes 429312 | tf_op jit(solution)/shard_map/reduce_sum | solution.py:273
  64.0 0.0 copy-done.8
  64.0 0.6 sqrt_add_fusion
  64.6 0.0 copy-done.4
  64.6 1.9 %divide_subtract_fusion = f32[26,32,128]{2,1,0:T(8,128)} fusion(f32[26,32,128]{2,1,0:T(8,128)S(1)} %copy-done.4, f32[26,32,128]{2,1,0:T(8,128)} %shard_map.112, f32[26,32]{1,0:T(8,128)S(1)} %get-tuple-element.9), kind=kLoop, calls=%fused_computation.6 | loop fusion | flops 319488 | bytes 1281280 | tf_op jit(solution)/shard_map/sub | solution.py:274
  66.6 1.3 %slice.20 = f32[256,1,128]{2,1,0:T(1,128)S(1)} slice(f32[256,27,128]{2,1,0:T(8,128)} %copy-done.1), slice={[0:256], [0:1], [0:128]} | slice | bytes 262144 | tf_op jit(solution)/shard_map/slice | solution.py:270
  67.9 0.1 copy.24
  68.0 0.9 %fusion.6 = bf16[256,128]{0,1:T(8,128)(2,1)S(1)} fusion(f32[256,479]{0,1:T(8,128)} %copy-done.2, f32[256,1,128]{0,2,1:T(8,128)S(1)} %copy.24), kind=kLoop, calls=%fused_computation.11 | loop fusion | flops 65536 | bytes 327680 | tf_op jit(solution)/shard_map/convert_element_type | solution.py:270
  68.9 0.7 %copy.22 = bf16[256,128]{1,0:T(8,128)(2,1)} copy(bf16[256,128]{0,1:T(8,128)(2,1)S(1)} %fusion.6) | data formatting | bytes 131072
  (1 shorter events, 0.0 us)
Async XLA Ops:
  0.6 1.2 %copy-start = (bf16[479,1024]{1,0:T(8,128)(2,1)S(1)}, bf16[479,1024]{1,0:T(8,128)(2,1)}, u32[]{:S(2)}) copy-start(bf16[479,1024]{1,0:T(8,128)(2,1)} %param.12) | copy-start | bytes 2942980
  0.6 3.5 %copy-start.3 = (bf16[351,729]{1,0:T(8,128)(2,1)S(1)}, bf16[351,729]{1,0:T(8,128)(2,1)}, u32[]{:S(2)}) copy-start(bf16[351,729]{1,0:T(8,128)(2,1)} %constant.76) | copy-start | bytes 1535278
  3.3 0.8 %copy-start.2 = (f32[256,479]{0,1:T(8,128)}, f32[256,479]{0,1:T(8,128)S(1)}, u32[]{:S(2)}) copy-start(f32[256,479]{0,1:T(8,128)S(1)} %fusion.29) | copy-start | bytes 1471492
  7.9 2.7 %copy-start.5 = (bf16[256,128]{1,0:T(8,128)(2,1)S(1)}, bf16[256,128]{1,0:T(8,128)(2,1)}, u32[]{:S(2)}) copy-start(bf16[256,128]{1,0:T(8,128)(2,1)} %param.10) | copy-start | bytes 196612
  11.4 2.5 %copy-start.1 = (f32[256,27,128]{2,1,0:T(8,128)}, f32[256,27,128]{2,1,0:T(8,128)S(1)}, u32[]{:S(2)}) copy-start(f32[256,27,128]{2,1,0:T(8,128)S(1)} %fusion) | copy-start | bytes 10616836
  12.0 2.0 %copy-start.6 = (s32[256,26]{0,1:T(8,128)S(1)}, s32[256,26]{0,1:T(8,128)}, u32[]{:S(2)}) copy-start(s32[256,26]{0,1:T(8,128)} %param.14) | copy-start | bytes 79876
  12.0 2.0 %copy-start.7 = (s32[256,26,1]{0,2,1:T(1,128)S(1)}, s32[256,26,1]{0,2,1:T(1,128)}, u32[]{:S(2)}) copy-start(s32[256,26,1]{0,2,1:T(1,128)} %param.13) | copy-start | bytes 79876
  14.0 50.0 %copy-start.8 = (f32[26,32]{1,0:T(8,128)S(1)}, f32[26,32]{1,0:T(8,128)}, u32[]{:S(2)}) copy-start(f32[26,32]{1,0:T(8,128)} %param.16) | copy-start | bytes 9988
  14.0 50.7 %copy-start.4 = (f32[26,32,128]{2,1,0:T(8,128)S(1)}, f32[26,32,128]{2,1,0:T(8,128)}, u32[]{:S(2)}) copy-start(f32[26,32,128]{2,1,0:T(8,128)} %param.15) | copy-start | bytes 1277956
where the time goes:
time: 70 us; the launch traced here: 69.6 us
  Pallas kernels  48.1 us (69%)
  local copies, waits for them, and re-layouts  13.3 us (19%)
  other arithmetic  4.78 us (7%)
  matrix products  2.67 us (4%)
  between operations  0.81 us (1%)
    pallas_call x1, Pallas kernels, route(): pl.pallas_call(functools.partial(route_kernel, chunks, z_count), out_shap...  48.1 us
    unnamed x22, local copies, waits for them, and re-layouts  7.39 us
    reshape x2, local copies, waits for them, and re-layouts, per_device(): symmetric = symmetric.reshape(batch_rows, feature_count, feature_count)  3.32 us
    sub x1, other arithmetic, per_device(): table - LEARN_RATE * row_grad / (jnp.sqrt(new_accum)[:, :, None] + EPSILON)  1.95 us
    dot_general x1, matrix products, per_device(): jnp.einsum('bh,zh->bz', top_cot, top_weight, preferred_element_type=jnp.f...  1.5 us

commit v1 on v0

v1 whole, which is shorter than its diff:
```python
import functools

import jax
import jax.numpy as jnp
from jax import lax
from jax.experimental import pallas as pl
from jax.experimental.pallas import tpu as pltpu
from jax.sharding import PartitionSpec as P

LEARN_RATE = 0.1
EPSILON = 1e-08
MESH = pl.DeviceIdType.MESH
VMEM_LIMIT = 60 * 1024 * 1024
LANES = 128
GROUP = 8
SPAN = 256


def table_slots(table_count, handlers, half):
    slots = []
    for start in range(0, table_count, handlers):
        count = min(handlers, table_count - start)
        if count == handlers:
            slots.append((start, None))
        else:
            step = handlers // count
            owners = [(i * step + (i % 2) * half) % handlers for i in range(count)]
            if len(set(owners)) < count:
                owners = list(range(count))
            slots.append((start, tuple(owners)))
    return slots


def step_kernel(
    slots, z_count, mp_count,
    sparse, dense, cot, weight, owner, local, table, accum,
    dense_out, table_out, accum_out,
    feats, cot_v, weight_v, owner_v, local_v, table_v, accum_v,
    keys, blocks, spread, top, grads, got_rows, got_keys,
    partial, own_sum, z_in, fin_out, fin_in, turned,
    load_sem, self_sem, key_send, key_recv, row_send, row_recv,
    z_send, z_recv, fin_send, fin_recv,
):
    table_count, batch_rows, width = sparse.shape
    rows_own = table.shape[1]
    handlers = 2 * mp_count
    rows_grp = rows_own * mp_count
    block = handlers * rows_own
    feature_count = table_count + 1
    dp, mp = lax.axis_index("dp"), lax.axis_index("mp")
    z, x = dp // 2, dp % 2
    me = x * mp_count + mp

    def plane_device(h):
        return (z * 2 + h // mp_count, h % mp_count)

    def z_device(d):
        return (((z + d) % z_count) * 2 + x, mp)

    loads = [
        pltpu.make_async_copy(source, target, load_sem.at[i])
        for i, (source, target) in enumerate((
            (cot, cot_v), (weight, weight_v), (owner, owner_v), (local, local_v),
            (sparse, feats.at[pl.ds(0, table_count)]), (dense, feats.at[table_count]),
            (table, table_v), (accum, accum_v),
        ))
    ]
    for load in loads:
        load.start()

    peers = [plane_device((me + d) % handlers) for d in range(1, handlers)]
    peers_z = [z_device(d) for d in range(1, z_count)]
    barrier = pltpu.get_barrier_semaphore()
    for device in peers + peers_z:
        pl.semaphore_signal(barrier, inc=1, device_id=device, device_id_type=MESH)

    started = []

    def begin(copy):
        copy.start()
        started.append(copy)
        return copy

    loads[0].wait()
    loads[1].wait()
    input_cot = lax.dot_general(
        cot_v[...], weight_v[...], (((1,), (1,)), ((), ())), preferred_element_type=jnp.float32
    )
    top[...] = input_cot[:, :width]
    pair_count = feature_count * (feature_count - 1) // 2
    feature_pad = SPAN // GROUP
    per_dot = LANES // feature_pad
    dots = -(-feature_count // per_dot)
    columns = lax.broadcasted_iota(jnp.int32, (1, dots * LANES), 1)
    left, right = columns // feature_pad, columns % feature_pad
    inside = (left < feature_count) & (right < feature_count) & (left != right)
    left = jnp.where(left == table_count, 0, left + 1)
    right = jnp.where(right == table_count, 0, right + 1)
    high, low = jnp.maximum(left, right), jnp.minimum(left, right)
    place = jnp.where(inside, high * (high - 1) // 2 + low, -1)
    pairs = lax.broadcasted_iota(jnp.int32, (pair_count, dots * LANES), 0)
    select = jnp.where(pairs == place, 1.0, 0.0).astype(jnp.bfloat16)
    symmetric = jnp.dot(
        input_cot[:, width:].astype(jnp.bfloat16), select, preferred_element_type=jnp.float32
    ).astype(jnp.bfloat16)
    rep_row = lax.broadcasted_iota(jnp.int32, (LANES, per_dot * SPAN), 0)
    rep_col = lax.broadcasted_iota(jnp.int32, (LANES, per_dot * SPAN), 1)
    repeat = jnp.where(rep_row == rep_col // GROUP, 1.0, 0.0).astype(jnp.bfloat16)

    loads[2].wait()
    loads[3].wait()
    for t in range(table_count):
        keys[t] = owner_v[t] * rows_grp + local_v[t : t + 1]

    loads[4].wait()
    loads[5].wait()

    def build_blocks(i, carry):
        span = pl.ds(pl.multiple_of(i * 2 * GROUP, 2 * GROUP), 2 * GROUP)
        both = feats[:, span, :].astype(jnp.float32)
        pad = jnp.zeros(((feature_pad - feature_count) * GROUP, width), jnp.float32)
        for half in range(2):
            part = both[:, half * GROUP : (half + 1) * GROUP, :]
            part = part.reshape(feature_count * GROUP, width)
            blocks[2 * i + half] = jnp.concatenate([part, pad], 0).astype(jnp.bfloat16)
        return carry

    lax.fori_loop(0, batch_rows // (2 * GROUP), build_blocks, 0)

    mask = (
        lax.broadcasted_iota(jnp.int32, (GROUP, SPAN), 1) % GROUP
        == lax.broadcasted_iota(jnp.int32, (GROUP, SPAN), 0)
    )

    def gradients(first, last):
        for q in range(first // per_dot, -(-last // per_dot)):
            spread[:, q * per_dot * SPAN : (q + 1) * per_dot * SPAN] = jnp.dot(
                symmetric[:, q * LANES : (q + 1) * LANES], repeat,
                preferred_element_type=jnp.float32,
            )

        def one(i, carry):
            outs = []
            for half in range(2):
                rows = pl.ds(pl.multiple_of((2 * i + half) * GROUP, GROUP), GROUP)
                parts = [
                    jnp.where(mask, spread[rows, t * SPAN : (t + 1) * SPAN], 0.0)
                    for t in range(first, last)
                ]
                lhs = jnp.concatenate(parts, 0).astype(jnp.bfloat16)
                outs.append(
                    jnp.dot(lhs, blocks[2 * i + half], preferred_element_type=jnp.float32)
                )
            span = pl.ds(pl.multiple_of(i * 2 * GROUP, 2 * GROUP), 2 * GROUP)
            for t in range(first, last):
                at = (t - first) * GROUP
                both = jnp.concatenate([out[at : at + GROUP] for out in outs], 0)
                if t == table_count:
                    dense_out[span, :] = (both + top[span, :]).astype(jnp.bfloat16)
                else:
                    grads[t, span, :] = both.astype(jnp.bfloat16)
            return carry

        lax.fori_loop(0, batch_rows // (2 * GROUP), one, 0)

    def row_copy(slot, t, d):
        return pltpu.make_async_remote_copy(
            src_ref=grads.at[t],
            dst_ref=got_rows.at[slot, me],
            send_sem=row_send.at[slot, d - 1],
            recv_sem=row_recv.at[slot, d - 1],
            device_id=plane_device((me + d) % handlers),
            device_id_type=MESH,
        )

    def key_copy(slot, t, d):
        return pltpu.make_async_remote_copy(
            src_ref=keys.at[t],
            dst_ref=got_keys.at[slot, me],
            send_sem=key_send.at[slot, d - 1],
            recv_sem=key_recv.at[slot, d - 1],
            device_id=plane_device((me + d) % handlers),
            device_id_type=MESH,
        )

    def self_copies(slot, t):
        return [
            pltpu.make_async_copy(grads.at[t], got_rows.at[slot, me], self_sem.at[slot, 0]),
            pltpu.make_async_copy(keys.at[t], got_keys.at[slot, me], self_sem.at[slot, 1]),
        ]

    def each_send(slot, action, kind):
        start, owners = slots[slot]
        make = row_copy if kind == "rows" else key_copy
        for d in range(1, handlers):
            target = (me + d) % handlers
            if owners is None:
                action(make(slot, start + target, d))
            else:
                for i, h in enumerate(owners):
                    @pl.when(target == h)
                    def _(i=i):
                        action(make(slot, start + i, d))

    def handled(slot, body):
        start, owners = slots[slot]
        if owners is None:
            body(start + me)
        else:
            for i, h in enumerate(owners):
                @pl.when(me == h)
                def _(i=i):
                    body(start + i)

    def send_slot(slot):
        each_send(slot, lambda copy: copy.start(), "keys")
        each_send(slot, lambda copy: copy.start(), "rows")

        def own(t):
            for copy in self_copies(slot, t):
                copy.start()

        handled(slot, own)

    def z_copy(slot, d):
        return pltpu.make_async_remote_copy(
            src_ref=partial.at[slot, d - 1],
            dst_ref=z_in.at[slot, d - 1],
            send_sem=z_send.at[slot, d - 1],
            recv_sem=z_recv.at[slot, d - 1],
            device_id=z_device(d),
            device_id_type=MESH,
        )

    lookups = handlers * batch_rows

    def job(slot):
        def body(t):
            for copy in self_copies(slot, t):
                copy.wait()
            for d in range(1, handlers):
                row_copy(slot, t, d).wait_recv()
                key_copy(slot, t, d).wait_recv()
            targets = lax.broadcasted_iota(jnp.int32, (block, batch_rows), 0)

            def sums(d):
                base = ((z + d) % z_count) * block
                total = jnp.zeros((block, width), jnp.float32)
                for h in range(handlers):
                    onehot = jnp.where(targets == got_keys[slot, h] - base, 1.0, 0.0)
                    total = total + jnp.dot(
                        onehot.astype(jnp.bfloat16), got_rows[slot, h],
                        preferred_element_type=jnp.float32,
                    )
                return total

            def away(step, carry):
                d = step + 1
                partial[slot, step] = sums(d).astype(jnp.bfloat16)
                z_copy(slot, d).start()
                return carry

            lax.fori_loop(0, z_count - 1, away, 0)
            own_sum[slot] = sums(0)

        handled(slot, body)

    def fin_copy(slot, t, d):
        target = (me + d) % handlers
        return pltpu.make_async_remote_copy(
            src_ref=fin_out.at[slot, target],
            dst_ref=fin_in.at[t],
            send_sem=fin_send.at[slot, d - 1],
            recv_sem=fin_recv.at[slot, d - 1],
            device_id=plane_device(target),
            device_id_type=MESH,
        )

    def finish(slot):
        def body(t):
            def wait(step, carry):
                z_copy(slot, step + 1).wait_recv()
                return carry

            lax.fori_loop(0, z_count - 1, wait, 0)
            total = own_sum[slot]
            for d in range(1, z_count):
                total = total + z_in[slot, d - 1].astype(jnp.float32)
            total = total.astype(jnp.bfloat16)
            for h in range(handlers):
                fin_out[slot, h] = total[h * rows_own : (h + 1) * rows_own]
            for d in range(1, handlers):
                fin_copy(slot, t, d).start()
            fin_in[t] = fin_out[slot, me]

        handled(slot, body)

    lane = lax.broadcasted_iota(jnp.int32, (rows_own, LANES), 1)
    state = {}

    def update(slot):
        start, owners = slots[slot]
        count = handlers if owners is None else len(owners)
        for d in range(1, handlers):
            source = (me - d + handlers) % handlers
            if owners is None:
                fin_copy(slot, start, d).wait_recv()
            else:
                for i, h in enumerate(owners):
                    @pl.when(source == h)
                    def _():
                        fin_copy(slot, start, d).wait_recv()
        for t in range(start, start + count):
            grad = fin_in[t].astype(jnp.float32)
            mean = jnp.sum(grad * grad, axis=1, keepdims=True) * (1.0 / width)
            new = state["old"][:, t : t + 1] + mean
            state["new"] = jnp.where(lane == t, new, state["new"])
            table_out[t] = table_v[t] - LEARN_RATE * grad / (jnp.sqrt(new) + EPSILON)

    def rows_of(slot):
        start, owners = slots[slot]
        return start, start + (handlers if owners is None else len(owners))

    count = len(slots)
    for slot in range(count):
        first, last = rows_of(slot)
        gradients(first, last + (1 if slot == count - 1 else 0))
        if slot == 0:
            pl.semaphore_wait(barrier, handlers - 1 + z_count - 1)
        send_slot(slot)

    loads[6].wait()
    loads[7].wait()
    old = jnp.concatenate(
        [accum_v[...], jnp.zeros((LANES - table_count, rows_own), jnp.float32)], 0
    )
    state["old"] = old.T
    state["new"] = jnp.zeros((rows_own, LANES), jnp.float32)

    for step in range(count + 2):
        if step < count:
            job(step)
        if 0 <= step - 1 < count:
            finish(step - 1)
        if 0 <= step - 2 < count:
            update(step - 2)
    accum_out[...] = state["new"].T[:table_count]

    for slot in range(count):
        each_send(slot, lambda copy: copy.wait_send(), "rows")
        each_send(slot, lambda copy: copy.wait_send(), "keys")

        def sent(t):
            def wait(step, carry):
                z_copy(slot, step + 1).wait_send()
                return carry

            lax.fori_loop(0, z_count - 1, wait, 0)
            for d in range(1, handlers):
                fin_copy(slot, t, d).wait_send()

        handled(slot, sent)


def per_device(sparse_vecs, dense_vec, top_cot, top_weight, owner_ids, local_rows, table, accum):
    batch_rows, table_count, width = sparse_vecs.shape
    rows_own = table.shape[1]
    z_count = lax.axis_size("dp") // 2
    mp_count = lax.axis_size("mp")
    handlers = 2 * mp_count
    slots = table_slots(table_count, handlers, mp_count // 2)
    count = len(slots)
    block = handlers * rows_own
    feature_count = table_count + 1
    dots = -(-feature_count * (SPAN // GROUP) // LANES)
    others = max(1, z_count - 1)
    near = handlers - 1
    any_spec = pl.BlockSpec(memory_space=pl.ANY)
    vmem = pl.BlockSpec(memory_space=pltpu.VMEM)
    dma = pltpu.SemaphoreType.DMA
    bf16, f32, i32 = jnp.bfloat16, jnp.float32, jnp.int32
    out_shape = (
        jax.ShapeDtypeStruct(dense_vec.shape, bf16),
        jax.ShapeDtypeStruct(table.shape, f32),
        jax.ShapeDtypeStruct(accum.shape, f32),
    )
    scratch = [
        pltpu.VMEM((feature_count, batch_rows, width), bf16),
        pltpu.VMEM(top_cot.shape, bf16),
        pltpu.VMEM(top_weight.shape, bf16),
        pltpu.VMEM((table_count, 1, batch_rows), i32),
        pltpu.VMEM((table_count, batch_rows), i32),
        pltpu.VMEM(table.shape, f32),
        pltpu.VMEM(accum.shape, f32),
        pltpu.VMEM((table_count, 1, batch_rows), i32),
        pltpu.VMEM((batch_rows // GROUP, SPAN, width), bf16),
        pltpu.VMEM((batch_rows, dots * (LANES // (SPAN // GROUP)) * SPAN), f32),
        pltpu.VMEM((batch_rows, width), f32),
        pltpu.VMEM((table_count, batch_rows, width), bf16),
        pltpu.VMEM((count, handlers, batch_rows, width), bf16),
        pltpu.VMEM((count, handlers, 1, batch_rows), i32),
        pltpu.VMEM((count, others, block, width), bf16),
        pltpu.VMEM((count, block, width), f32),
        pltpu.VMEM((count, others, block, width), bf16),
        pltpu.VMEM((count, handlers, rows_own, width), bf16),
        pltpu.VMEM((table_count, rows_own, width), bf16),
        pltpu.VMEM((rows_own, LANES), f32),
        dma((8,)),
        dma((count, 2)),
        dma((count, near)),
        dma((count, near)),
        dma((count, near)),
        dma((count, near)),
        dma((count, others)),
        dma((count, others)),
        dma((count, near)),
        dma((count, near)),
    ]
    return pl.pallas_call(
        functools.partial(step_kernel, slots, z_count, mp_count),
        out_shape=out_shape,
        in_specs=[any_spec] * 8,
        out_specs=(vmem,) * 3,
        scratch_shapes=scratch,
        compiler_params=pltpu.CompilerParams(
            collective_id=0, has_side_effects=True, vmem_limit_bytes=VMEM_LIMIT
        ),
    )(
        sparse_vecs.transpose(1, 0, 2), dense_vec, top_cot, top_weight,
        owner_ids.transpose(1, 2, 0), local_rows.T, table, accum,
    )


def solution(mesh):
    in_specs = (
        P(("dp", "mp"), None, None),
        P(("dp", "mp"), None),
        P(("dp", "mp"), None),
        P(),
        P(("dp", "mp"), None, None),
        P(("dp", "mp"), None),
        P(None, ("dp", "mp"), None),
        P(None, ("dp", "mp")),
    )
    out_specs = (P(("dp", "mp"), None), P(None, ("dp", "mp"), None), P(None, ("dp", "mp")))
    return jax.shard_map(
        per_device, mesh=mesh, in_specs=in_specs, out_specs=out_specs, check_vma=False
    )
```

time: 70 us -> 52.1 us (0.74)
  local copies, waits for them, and re-layouts: 13.3 us -> 4.59 us
  other arithmetic: 4.78 us -> 0 us
  matrix products: 2.67 us -> 0 us
  Pallas kernels: 48.1 us -> 46.6 us
    reshape x2 -> x0, local copies, waits for them, and re-layouts: 3.32 us -> none  [per_device(): symmetric = symmetric.reshape(batch_rows, feature_count, feature_count)]
    unnamed x22 -> x3, local copies, waits for them, and re-layouts: 7.39 us -> 4.59 us
    dot_general x3 -> x0, matrix products: 2.67 us -> none  [the longest x1 1.5 us: per_device(): jnp.einsum('bh,zh->bz', top_cot, top_weight, preferred_element_type=jnp.f...]
    sub x1 -> x0, other arithmetic: 1.95 us -> none  [per_device(): table - LEARN_RATE * row_grad / (jnp.sqrt(new_accum)[:, :, None] + EPSILON)]
    slice x2 -> x0, local copies, waits for them, and re-layouts: 1.85 us -> none  [the longest x1 1.29 us: per_device(): feature_grad[:, 0]]
    pallas_call x1, Pallas kernels: 48.1 us -> 46.6 us  [per_device(): pl.pallas_call(functools.partial(step_kernel, slots, z_count, mp_count),...]
    reduce_sum x1 -> x0, other arithmetic: 1.19 us -> none  [per_device(): new_accum = accum + jnp.mean(row_grad * row_grad, axis=-1)]
    convert_element_type x1 -> x0, other arithmetic: 0.92 us -> none  [per_device(): (input_cot[:, :row_width] + feature_grad[:, 0]).astype(jnp.bfloat16)]
where the time goes in v1:
time: 52.1 us; the launch traced here: 51.9 us
  Pallas kernels  46.6 us (89%)
  local copies, waits for them, and re-layouts  4.59 us (9%)
  between operations  0.64 us (1%)
    pallas_call x1, Pallas kernels, per_device(): pl.pallas_call(functools.partial(step_kernel, slots, z_count, mp_count),...  46.6 us
    unnamed x3, local copies, waits for them, and re-layouts  4.59 us

profile of v1, /device:TPU:0, one launch (start us, length us, event | category | flops | bytes accessed | tf_op | source)
XLA Modules:
  0.0 51.9 jit_solution(16561729289043324491)
XLA Ops:
  0.6 46.6 %shard_map.103 = (bf16[256,128]{1,0:T(8,128)(2,1)}, f32[26,32,128]{2,1,0:T(8,128)}, f32[26,32]{1,0:T(8,128)}) custom-call(bf16[26,256,128]{2,1,0:T(8,128)(2,1)} %bitcast.3, bf16[256,128]{1,0:T(8,128)(2,1)} %dense.1, bf16[256,1024]{1,0:T(8,128)(2,1)} %cot.1, bf16[479,1024]{1,0:T(8,128)(2,1)} %weight.1, s32[26,1,256]{2,1,0:T(1,128)} %bitcast.5, ...), custom_call_target="tpu_custom_call" | custom-call | tf_op jit(solution)/shard_map/pallas_call | solution.py:419
  47.3 1.5 %copy.14 = bf16[256,128]{1,0:T(8,128)(2,1)} copy(bf16[256,128]{1,0:T(8,128)(2,1)} %get-tuple-element.6) | data formatting | bytes 131072
  48.7 1.8 %copy.15 = f32[26,32,128]{2,1,0:T(8,128)} copy(f32[26,32,128]{2,1,0:T(8,128)} %get-tuple-element.7) | data formatting | bytes 851968
  50.5 1.3 %copy.16 = f32[26,32]{1,0:T(8,128)} copy(f32[26,32]{1,0:T(8,128)} %get-tuple-element.8) | data formatting | bytes 6656

commit v2 on v1

v2 whole, which is shorter than its diff:
```python
import functools

import jax
import jax.numpy as jnp
from jax import lax
from jax.experimental import pallas as pl
from jax.experimental.pallas import tpu as pltpu
from jax.sharding import PartitionSpec as P

LEARN_RATE = 0.1
EPSILON = 1e-08
MESH = pl.DeviceIdType.MESH
VMEM_LIMIT = 60 * 1024 * 1024
LANES = 128
GROUP = 8
SPAN = 256
UNROLL = 4
PARTS = (2, 14, 26)


def table_slots(table_count, handlers):
    slots = []
    rest = table_count % handlers
    starts = [0] * (rest > 0) + list(range(rest, table_count, handlers))
    for start in starts:
        count = rest if rest and start == 0 else handlers
        if count == handlers:
            slots.append((start, None))
        else:
            step = 2 if 2 * count <= handlers else 1
            owners = [handlers - step * (count - i) for i in range(count)]
            slots.append((start, tuple(owners)))
    return slots


def step_kernel(
    slots, z_count, mp_count,
    sparse, dense, cot, weight, owner, local, table, accum,
    dense_out, table_out, accum_out,
    feats, cot_v, weight_v, owner_v, local_v, table_v, accum_v,
    keys, select, repeat, blocks, spread, top, grads, got_rows, got_keys,
    partial, own_sum, z_in, fin_out, fin_in,
    load_sem, self_sem, key_send, key_recv, row_send, row_recv,
    z_send, z_recv, fin_send, fin_recv,
):
    table_count, batch_rows, width = sparse.shape
    rows_own = table.shape[1]
    handlers = 2 * mp_count
    rows_grp = rows_own * mp_count
    block = handlers * rows_own
    feature_count = table_count + 1
    dp, mp = lax.axis_index("dp"), lax.axis_index("mp")
    z, x = dp // 2, dp % 2
    me = x * mp_count + mp

    def plane_device(h):
        return (z * 2 + h // mp_count, h % mp_count)

    def z_device(d):
        return (((z + d) % z_count) * 2 + x, mp)

    loads = [
        pltpu.make_async_copy(source, target, load_sem.at[i])
        for i, (source, target) in enumerate((
            (cot, cot_v), (weight, weight_v), (owner, owner_v), (local, local_v),
            (sparse, feats.at[pl.ds(0, table_count)]), (dense, feats.at[table_count]),
            (table, table_v), (accum, accum_v),
        ))
    ]
    for load in loads:
        load.start()

    peers = [plane_device((me + d) % handlers) for d in range(1, handlers)]
    peers_z = [z_device(d) for d in range(1, z_count)]
    barrier = pltpu.get_barrier_semaphore()
    for device in peers + peers_z:
        pl.semaphore_signal(barrier, inc=1, device_id=device, device_id_type=MESH)

    with jax.named_scope("const"):
        pair_count = feature_count * (feature_count - 1) // 2
        feature_pad = SPAN // GROUP
        per_dot = LANES // feature_pad
        dots = -(-feature_count // per_dot)
        columns = lax.broadcasted_iota(jnp.int32, (1, dots * LANES), 1)
        left, right = columns // feature_pad, columns % feature_pad
        inside = (left < feature_count) & (right < feature_count) & (left != right)
        left = jnp.where(left == table_count, 0, left + 1)
        right = jnp.where(right == table_count, 0, right + 1)
        high, low = jnp.maximum(left, right), jnp.minimum(left, right)
        place = jnp.where(inside, high * (high - 1) // 2 + low, -1)
        pairs = lax.broadcasted_iota(jnp.int32, (pair_count, dots * LANES), 0)
        select[...] = jnp.where(pairs == place, 1.0, 0.0).astype(jnp.bfloat16)
        rep_row = lax.broadcasted_iota(jnp.int32, (LANES, per_dot * SPAN), 0)
        rep_col = lax.broadcasted_iota(jnp.int32, (LANES, per_dot * SPAN), 1)
        repeat[...] = jnp.where(rep_row == rep_col // GROUP, 1.0, 0.0).astype(jnp.bfloat16)
    with jax.named_scope("loadwait"):
        loads[0].wait()
        loads[1].wait()
    input_cot = lax.dot_general(
        cot_v[...], weight_v[...], (((1,), (1,)), ((), ())), preferred_element_type=jnp.float32
    )
    top[...] = input_cot[:, :width]
    symmetric = jnp.dot(
        input_cot[:, width:].astype(jnp.bfloat16), select[...], preferred_element_type=jnp.float32
    ).astype(jnp.bfloat16)

    loads[4].wait()
    loads[5].wait()

    def build_blocks(i, carry):
        span = pl.ds(pl.multiple_of(i * 2 * GROUP, 2 * GROUP), 2 * GROUP)
        both = feats[:, span, :].astype(jnp.float32)
        pad = jnp.zeros(((feature_pad - feature_count) * GROUP, width), jnp.float32)
        for half in range(2):
            part = both[:, half * GROUP : (half + 1) * GROUP, :]
            part = part.reshape(feature_count * GROUP, width)
            blocks[2 * i + half] = jnp.concatenate([part, pad], 0).astype(jnp.bfloat16)
        return carry

    with jax.named_scope("blocks"):
        lax.fori_loop(0, batch_rows // (2 * GROUP), build_blocks, 0)

    mask = (
        lax.broadcasted_iota(jnp.int32, (GROUP, SPAN), 1) % GROUP
        == lax.broadcasted_iota(jnp.int32, (GROUP, SPAN), 0)
    )

    def gradients(first, last):
        for q in range(first // per_dot, -(-last // per_dot)):
            spread[:, q * per_dot * SPAN : (q + 1) * per_dot * SPAN] = jnp.dot(
                symmetric[:, q * LANES : (q + 1) * LANES], repeat[...],
                preferred_element_type=jnp.float32,
            )

        def one(step, carry):
            for i in [step * UNROLL + u for u in range(UNROLL)]:
                outs = []
                for half in range(2):
                    rows = pl.ds(pl.multiple_of((2 * i + half) * GROUP, GROUP), GROUP)
                    parts = [
                        jnp.where(mask, spread[rows, t * SPAN : (t + 1) * SPAN], 0.0)
                        for t in range(first, last)
                    ]
                    lhs = jnp.concatenate(parts, 0).astype(jnp.bfloat16)
                    outs.append(
                        jnp.dot(lhs, blocks[2 * i + half], preferred_element_type=jnp.float32)
                    )
                span = pl.ds(pl.multiple_of(i * 2 * GROUP, 2 * GROUP), 2 * GROUP)
                for t in range(first, last):
                    at = (t - first) * GROUP
                    both = jnp.concatenate([out[at : at + GROUP] for out in outs], 0)
                    if t == table_count:
                        dense_out[span, :] = (both + top[span, :]).astype(jnp.bfloat16)
                    else:
                        grads[t, span, :] = both.astype(jnp.bfloat16)
            return carry

        lax.fori_loop(0, batch_rows // (2 * GROUP * UNROLL), one, 0)

    def table_of(slot, h):
        return slots[slot][0] + h // 2 + (h % 2) * (handlers // 2)

    def row_copy(slot, t, target, source):
        return pltpu.make_async_remote_copy(
            src_ref=grads.at[t],
            dst_ref=got_rows.at[slot, source],
            send_sem=row_send.at[slot, target],
            recv_sem=row_recv.at[slot, source],
            device_id=plane_device(target),
            device_id_type=MESH,
        )

    def key_copy(target, source):
        return pltpu.make_async_remote_copy(
            src_ref=keys.at[target],
            dst_ref=got_keys.at[source],
            send_sem=key_send.at[target],
            recv_sem=key_recv.at[source],
            device_id=plane_device(target),
            device_id_type=MESH,
        )

    def self_copy(slot, t):
        return pltpu.make_async_copy(grads.at[t], got_rows.at[slot, me], self_sem.at[slot])

    def targets_of(slot, parity):
        start, owners = slots[slot]
        if owners is None:
            for j in range(1, handlers // 2):
                h = 2 * ((me // 2 + j) % (handlers // 2)) + parity
                yield h, table_of(slot, h), None
            h = 2 * (me // 2) + parity
            yield h, table_of(slot, h), me != h
        else:
            for i, h in enumerate(owners):
                if h % 2 == parity:
                    yield h, start + i, me != h

    def guarded(condition, body):
        if condition is None:
            body()
        else:
            pl.when(condition)(body)

    def handled(slot, body, parity=None):
        start, owners = slots[slot]
        if owners is None:
            if parity is None:
                body(table_of(slot, me))
            else:
                guarded(me % 2 == parity, lambda: body(table_of(slot, me)))
        else:
            for i, h in enumerate(owners):
                if parity is None or h % 2 == parity:
                    guarded(me == h, lambda i=i: body(start + i))

    def send_rows(slot, parity):
        for h, t, condition in targets_of(slot, parity):
            guarded(condition, lambda: row_copy(slot, t, h, me).start())
        handled(slot, lambda t: self_copy(slot, t).start(), parity)

    def build_keys():
        for slot, (start, owners) in enumerate(slots):
            for h in range(handlers):
                if owners is None:
                    t = table_of(slot, h)
                else:
                    t = start + (owners.index(h) if h in owners else 0)
                keys[h, slot] = owner_v[t] * rows_grp + local_v[t : t + 1]
        for slot in range(len(slots)):
            got_keys[me, slot] = keys[me, slot]

    def send_keys():
        for d in range(1, handlers):
            key_copy((me + d) % handlers, me).start()

    def wait_sent(slot):
        for parity in range(2):
            for h, t, condition in targets_of(slot, parity):
                guarded(condition, lambda: row_copy(slot, t, h, me).wait_send())

    def z_order(step):
        low = z_count - 1 - step
        low = low - jnp.where(low <= z, 1, 0)
        high = step + jnp.where(step >= z, 1, 0)
        return jnp.where(2 * z < z_count, low, high)

    def z_copy(slot, target, source):
        return pltpu.make_async_remote_copy(
            src_ref=partial.at[slot, target],
            dst_ref=z_in.at[slot, source],
            send_sem=z_send.at[slot, target],
            recv_sem=z_recv.at[slot, source],
            device_id=(target * 2 + x, mp),
            device_id_type=MESH,
        )

    def job(slot):
        def body(t):
            with jax.named_scope(f"jobwait{slot}"):
                self_copy(slot, t).wait()
                for d in range(1, handlers):
                    source = (me + d) % handlers
                    row_copy(slot, t, source, source).wait_recv()
            targets = lax.broadcasted_iota(jnp.int32, (block, batch_rows), 0)

            def sums(target):
                base = target * block
                total = jnp.zeros((block, width), jnp.float32)
                for h in range(handlers):
                    onehot = jnp.where(targets == got_keys[h, slot] - base, 1.0, 0.0)
                    total = total + jnp.dot(
                        onehot.astype(jnp.bfloat16), got_rows[slot, h],
                        preferred_element_type=jnp.float32,
                    )
                return total

            def away(step, carry):
                target = z_order(step)
                partial[slot, target] = sums(target).astype(jnp.bfloat16)
                z_copy(slot, target, z).start()
                return carry

            lax.fori_loop(0, z_count - 1, away, 0)
            own_sum[slot] = sums(z)

        handled(slot, body)

    def fin_copy(slot, t, target, source):
        return pltpu.make_async_remote_copy(
            src_ref=fin_out.at[slot, target],
            dst_ref=fin_in.at[t],
            send_sem=fin_send.at[slot, target],
            recv_sem=fin_recv.at[slot, source],
            device_id=plane_device(target),
            device_id_type=MESH,
        )

    def finish(slot):
        def body(t):
            def wait(step, carry):
                source = (z + 1 + step) % z_count
                z_copy(slot, source, source).wait_recv()
                return carry

            with jax.named_scope(f"finwait{slot}"):
                lax.fori_loop(0, z_count - 1, wait, 0)
            total = own_sum[slot]
            for d in range(1, z_count):
                total = total + z_in[slot, (z + d) % z_count].astype(jnp.float32)
            total = total.astype(jnp.bfloat16)
            for h in range(handlers):
                fin_out[slot, h] = total[h * rows_own : (h + 1) * rows_own]
            for d in range(1, handlers):
                fin_copy(slot, t, (me + d) % handlers, me).start()
            fin_in[t] = fin_out[slot, me]

        handled(slot, body)

    lane = lax.broadcasted_iota(jnp.int32, (rows_own, LANES), 1)
    state = {}

    def update(slot):
        start, owners = slots[slot]
        count = handlers if owners is None else len(owners)
        if owners is None:
            for d in range(1, handlers):
                source = (me + d) % handlers
                fin_copy(slot, table_of(slot, source), source, source).wait_recv()
        else:
            for i, h in enumerate(owners):
                guarded(me != h, lambda: fin_copy(slot, start + i, h, h).wait_recv())
        span = slice(start, start + count)
        grad = fin_in[span].astype(jnp.float32)
        mean = jnp.sum(grad * grad, axis=2, keepdims=True) * (1.0 / width)
        old = jnp.stack([state["old"][:, t : t + 1] for t in range(start, start + count)])
        new = old + mean
        for i in range(count):
            state["new"] = jnp.where(lane == start + i, new[i], state["new"])
        table_out[span] = table_v[span] - grad * (LEARN_RATE / (jnp.sqrt(new) + EPSILON))

    def rows_of(slot):
        start, owners = slots[slot]
        return start, start + (handlers if owners is None else len(owners))

    count = len(slots)
    sends = []
    for slot in range(count):
        first, last = rows_of(slot)
        if slots[slot][1] is None:
            sends += [(slot, 0, first + handlers // 2), (slot, 1, last)]
        else:
            sends += [(slot, 0, last), (slot, 1, last)]
    done = 0
    for part, last in enumerate(PARTS):
        last = min(last, table_count)
        if part == len(PARTS) - 1:
            last = table_count
        with jax.named_scope(f"grad{part}"):
            gradients(done, last + (1 if last == table_count else 0))
        if part == 0:
            loads[2].wait()
            loads[3].wait()
            build_keys()
            with jax.named_scope("barrier"):
                pl.semaphore_wait(barrier, handlers - 1 + z_count - 1)
            send_keys()
        for slot, parity, ready in sends:
            if done < ready <= last or (parity and ready == last == table_count):
                send_rows(slot, parity)
        done = last

    loads[6].wait()
    loads[7].wait()
    old = jnp.concatenate(
        [accum_v[...], jnp.zeros((LANES - table_count, rows_own), jnp.float32)], 0
    )
    state["old"] = old.T
    state["new"] = jnp.zeros((rows_own, LANES), jnp.float32)

    for d in range(1, handlers):
        source = (me + d) % handlers
        key_copy(source, source).wait_recv()

    plan = []
    for step in range(count + 1):
        plan += [(job, step)] * (step < count) + [(finish, step - 1)] * (step > 0)
    last = plan.pop()
    plan += [(update, slot) for slot in range(count - 2)] + [last]
    plan += [(update, slot) for slot in range(max(0, count - 2), count)]
    for stage, slot in plan:
        with jax.named_scope(f"{stage.__name__}{slot}"):
            stage(slot)
    with jax.named_scope("accum"):
        accum_out[...] = state["new"].T[:table_count]

    for d in range(1, handlers):
        key_copy((me + d) % handlers, me).wait_send()
    for slot in range(count):
      with jax.named_scope("sent"):
        wait_sent(slot)

        def sent(t):
            def wait(step, carry):
                target = (z + 1 + step) % z_count
                z_copy(slot, target, z).wait_send()
                return carry

            lax.fori_loop(0, z_count - 1, wait, 0)
            for d in range(1, handlers):
                fin_copy(slot, t, (me + d) % handlers, me).wait_send()

        handled(slot, sent)


def emit_kernel(*refs):
    sources, targets, sem = refs[:3], refs[3:6], refs[6]
    copies = [
        pltpu.make_async_copy(source, target, sem.at[i])
        for i, (source, target) in enumerate(zip(sources, targets))
    ]
    for copy in copies:
        copy.start()
    for copy in copies:
        copy.wait()


def per_device(sparse_vecs, dense_vec, top_cot, top_weight, owner_ids, local_rows, table, accum):
    batch_rows, table_count, width = sparse_vecs.shape
    rows_own = table.shape[1]
    z_count = lax.axis_size("dp") // 2
    mp_count = lax.axis_size("mp")
    handlers = 2 * mp_count
    slots = table_slots(table_count, handlers)
    count = len(slots)
    block = handlers * rows_own
    feature_count = table_count + 1
    dots = -(-feature_count * (SPAN // GROUP) // LANES)
    any_spec = pl.BlockSpec(memory_space=pl.ANY)
    hbm = pl.BlockSpec(memory_space=pltpu.HBM)
    vmem = pl.BlockSpec(memory_space=pltpu.VMEM)
    dma = pltpu.SemaphoreType.DMA
    bf16, f32, i32 = jnp.bfloat16, jnp.float32, jnp.int32
    out_shape = (
        jax.ShapeDtypeStruct(dense_vec.shape, bf16),
        jax.ShapeDtypeStruct(table.shape, f32),
        jax.ShapeDtypeStruct(accum.shape, f32),
    )
    scratch = [
        pltpu.VMEM((feature_count, batch_rows, width), bf16),
        pltpu.VMEM(top_cot.shape, bf16),
        pltpu.VMEM(top_weight.shape, bf16),
        pltpu.VMEM((table_count, 1, batch_rows), i32),
        pltpu.VMEM((table_count, batch_rows), i32),
        pltpu.VMEM(table.shape, f32),
        pltpu.VMEM(accum.shape, f32),
        pltpu.VMEM((handlers, count, 1, batch_rows), i32),
        pltpu.VMEM((feature_count * table_count // 2, dots * LANES), bf16),
        pltpu.VMEM((LANES, LANES // (SPAN // GROUP) * SPAN), bf16),
        pltpu.VMEM((batch_rows // GROUP, SPAN, width), bf16),
        pltpu.VMEM((batch_rows, dots * (LANES // (SPAN // GROUP)) * SPAN), f32),
        pltpu.VMEM((batch_rows, width), f32),
        pltpu.VMEM((table_count, batch_rows, width), bf16),
        pltpu.VMEM((count, handlers, batch_rows, width), bf16),
        pltpu.VMEM((handlers, count, 1, batch_rows), i32),
        pltpu.VMEM((count, z_count, block, width), bf16),
        pltpu.VMEM((count, block, width), f32),
        pltpu.VMEM((count, z_count, block, width), bf16),
        pltpu.VMEM((count, handlers, rows_own, width), bf16),
        pltpu.VMEM((table_count, rows_own, width), bf16),
        dma((8,)),
        dma((count,)),
        dma((handlers,)),
        dma((handlers,)),
        dma((count, handlers)),
        dma((count, handlers)),
        dma((count, z_count)),
        dma((count, z_count)),
        dma((count, handlers)),
        dma((count, handlers)),
    ]
    results = pl.pallas_call(
        functools.partial(step_kernel, slots, z_count, mp_count),
        out_shape=tuple(pltpu.VMEM(a.shape, a.dtype) for a in out_shape),
        in_specs=[hbm] * 8,
        out_specs=(vmem,) * 3,
        scratch_shapes=scratch,
        compiler_params=pltpu.CompilerParams(
            collective_id=0, has_side_effects=True, vmem_limit_bytes=VMEM_LIMIT
        ),
    )(
        sparse_vecs.transpose(1, 0, 2), dense_vec, top_cot, top_weight,
        owner_ids.transpose(1, 2, 0), local_rows.T, table, accum,
    )
    return pl.pallas_call(
        emit_kernel,
        out_shape=out_shape,
        in_specs=[vmem] * 3,
        out_specs=(any_spec,) * 3,
        scratch_shapes=[dma((3,))],
        compiler_params=pltpu.CompilerParams(vmem_limit_bytes=2 * 1024 * 1024),
    )(*results)


def solution(mesh):
    in_specs = (
        P(("dp", "mp"), None, None),
        P(("dp", "mp"), None),
        P(("dp", "mp"), None),
        P(),
        P(("dp", "mp"), None, None),
        P(("dp", "mp"), None),
        P(None, ("dp", "mp"), None),
        P(None, ("dp", "mp")),
    )
    out_specs = (P(("dp", "mp"), None), P(None, ("dp", "mp"), None), P(None, ("dp", "mp")))
    return jax.shard_map(
        per_device, mesh=mesh, in_specs=in_specs, out_specs=out_specs, check_vma=False
    )
```

time: 52.1 us -> 40.9 us (0.79)
  Pallas kernels: 46.6 us -> 40.2 us
  local copies, waits for them, and re-layouts: 4.59 us -> 0 us
    pallas_call x1, Pallas kernels: 46.6 us -> 39.3 us  [per_device(): pl.pallas_call(functools.partial(step_kernel, slots, z_count, mp_count),...]
    unnamed x3 -> x0, local copies, waits for them, and re-layouts: 4.59 us -> none
    pallas_call x0 -> x1, Pallas kernels: none -> 0.81 us  [per_device(): pl.pallas_call(emit_kernel, out_shape=out_shape, in_specs=[vmem] * 3, out...]
where the time goes in v2:
time: 40.9 us; the launch traced here: 40.8 us
  Pallas kernels  40.2 us (98%)
  between operations  0.64 us (2%)
    pallas_call x1, Pallas kernels, per_device(): pl.pallas_call(functools.partial(step_kernel, slots, z_count, mp_count),...  39.3 us

profile of v2, /device:TPU:0, one launch (start us, length us, event | category | flops | bytes accessed | tf_op | source)
XLA Modules:
  0.0 40.8 jit_solution(17743498619567086059)
XLA Ops:
  0.6 39.3 %shard_map.103 = (bf16[256,128]{1,0:T(8,128)(2,1)S(1)}, f32[26,32,128]{2,1,0:T(8,128)S(1)}, f32[26,32]{1,0:T(8,128)S(1)}) custom-call(bf16[26,256,128]{2,1,0:T(8,128)(2,1)} %bitcast.3, bf16[256,128]{1,0:T(8,128)(2,1)} %dense.1, bf16[256,1024]{1,0:T(8,128)(2,1)} %cot.1, bf16[479,1024]{1,0:T(8,128)(2,1)} %weight.1, s32[26,1,256]{2,1,0:T(1,128)} %bitcast.5, ...), custom_call_target="tpu_custom_call" | custom-call | tf_op jit(solution)/shard_map/pallas_call | solution.py:482
  40.0 0.8 %shard_map.104 = (bf16[256,128]{1,0:T(8,128)(2,1)}, f32[26,32,128]{2,1,0:T(8,128)}, f32[26,32]{1,0:T(8,128)}) custom-call(bf16[256,128]{1,0:T(8,128)(2,1)S(1)} %get-tuple-element.6.refs_0_, f32[26,32,128]{2,1,0:T(8,128)S(1)} %get-tuple-element.7.refs_1_, f32[26,32]{1,0:T(8,128)S(1)} %get-tuple-element.8.refs_2_), custom_call_target="tpu_custom_call" | custom-call | tf_op jit(solution)/shard_map/pallas_call | solution.py:495

commit v3 on v2

--- a/solution.py
+++ b/solution.py
@@ -40,7 +40,7 @@
     feats, cot_v, weight_v, owner_v, local_v, table_v, accum_v,
     keys, select, repeat, blocks, spread, top, grads, got_rows, got_keys,
     partial, own_sum, z_in, fin_out, fin_in,
-    load_sem, self_sem, key_send, key_recv, row_send, row_recv,
+    load_sem, key_send, key_recv, row_send, row_recv,
     z_send, z_recv, fin_send, fin_recv,
 ):
     table_count, batch_rows, width = sparse.shape
@@ -160,12 +160,15 @@
     def table_of(slot, h):
         return slots[slot][0] + h // 2 + (h % 2) * (handlers // 2)
 
+    def all_in(buffer, sem):
+        pltpu.make_async_copy(buffer, buffer, sem).wait()
+
     def row_copy(slot, t, target, source):
         return pltpu.make_async_remote_copy(
             src_ref=grads.at[t],
             dst_ref=got_rows.at[slot, source],
-            send_sem=row_send.at[slot, target],
-            recv_sem=row_recv.at[slot, source],
+            send_sem=row_send.at[slot],
+            recv_sem=row_recv.at[slot],
             device_id=plane_device(target),
             device_id_type=MESH,
         )
@@ -174,14 +177,14 @@
         return pltpu.make_async_remote_copy(
             src_ref=keys.at[target],
             dst_ref=got_keys.at[source],
-            send_sem=key_send.at[target],
-            recv_sem=key_recv.at[source],
+            send_sem=key_send,
+            recv_sem=key_recv,
             device_id=plane_device(target),
             device_id_type=MESH,
         )
 
     def self_copy(slot, t):
-        return pltpu.make_async_copy(grads.at[t], got_rows.at[slot, me], self_sem.at[slot])
+        return pltpu.make_async_copy(grads.at[t], got_rows.at[slot, me], row_recv.at[slot])
 
     def targets_of(slot, parity):
         start, owners = slots[slot]
@@ -235,9 +238,19 @@
             key_copy((me + d) % handlers, me).start()
 
     def wait_sent(slot):
-        for parity in range(2):
-            for h, t, condition in targets_of(slot, parity):
-                guarded(condition, lambda: row_copy(slot, t, h, me).wait_send())
+        start, owners = slots[slot]
+        if owners is None:
+            all_in(grads.at[pl.ds(0, handlers - 1)], row_send.at[slot])
+        else:
+            mine = [me == h for h in owners]
+            mine = functools.reduce(jnp.logical_or, mine)
+            for less in range(2):
+                sent = len(owners) - less
+                if sent:
+                    guarded(
+                        mine if less else jnp.logical_not(mine),
+                        lambda: all_in(grads.at[pl.ds(0, sent)], row_send.at[slot]),
+                    )
 
     def z_order(step):
         low = z_count - 1 - step
@@ -249,8 +262,8 @@
         return pltpu.make_async_remote_copy(
             src_ref=partial.at[slot, target],
             dst_ref=z_in.at[slot, source],
-            send_sem=z_send.at[slot, target],
-            recv_sem=z_recv.at[slot, source],
+            send_sem=z_send.at[slot],
+            recv_sem=z_recv.at[slot],
             device_id=(target * 2 + x, mp),
             device_id_type=MESH,
         )
@@ -258,10 +271,7 @@
     def job(slot):
         def body(t):
             with jax.named_scope(f"jobwait{slot}"):
-                self_copy(slot, t).wait()
-                for d in range(1, handlers):
-                    source = (me + d) % handlers
-                    row_copy(slot, t, source, source).wait_recv()
+                all_in(got_rows.at[slot], row_recv.at[slot])
             targets = lax.broadcasted_iota(jnp.int32, (block, batch_rows), 0)
 
             def sums(target):
@@ -290,21 +300,17 @@
         return pltpu.make_async_remote_copy(
             src_ref=fin_out.at[slot, target],
             dst_ref=fin_in.at[t],
-            send_sem=fin_send.at[slot, target],
-            recv_sem=fin_recv.at[slot, source],
+            send_sem=fin_send.at[slot],
+            recv_sem=fin_recv.at[slot],
             device_id=plane_device(target),
             device_id_type=MESH,
         )
 
     def finish(slot):
         def body(t):
-            def wait(step, carry):
-                source = (z + 1 + step) % z_count
-                z_copy(slot, source, source).wait_recv()
-                return carry
-
             with jax.named_scope(f"finwait{slot}"):
-                lax.fori_loop(0, z_count - 1, wait, 0)
+                if z_count > 1:
+                    all_in(z_in.at[slot, pl.ds(0, z_count - 1)], z_recv.at[slot])
             total = own_sum[slot]
             for d in range(1, z_count):
                 total = total + z_in[slot, (z + d) % z_count].astype(jnp.float32)
@@ -324,12 +330,16 @@
         start, owners = slots[slot]
         count = handlers if owners is None else len(owners)
         if owners is None:
-            for d in range(1, handlers):
-                source = (me + d) % handlers
-                fin_copy(slot, table_of(slot, source), source, source).wait_recv()
-        else:
-            for i, h in enumerate(owners):
-                guarded(me != h, lambda: fin_copy(slot, start + i, h, h).wait_recv())
+            all_in(fin_in.at[pl.ds(0, handlers - 1)], fin_recv.at[slot])
+        else:
+            mine = functools.reduce(jnp.logical_or, [me == h for h in owners])
+            for less in range(2):
+                came = count - less
+                if came:
+                    guarded(
+                        mine if less else jnp.logical_not(mine),
+                        lambda: all_in(fin_in.at[pl.ds(0, came)], fin_recv.at[slot]),
+                    )
         span = slice(start, start + count)
         grad = fin_in[span].astype(jnp.float32)
         mean = jnp.sum(grad * grad, axis=2, keepdims=True) * (1.0 / width)
@@ -378,9 +388,7 @@
     state["old"] = old.T
     state["new"] = jnp.zeros((rows_own, LANES), jnp.float32)
 
-    for d in range(1, handlers):
-        source = (me + d) % handlers
-        key_copy(source, source).wait_recv()
+    all_in(got_keys.at[pl.ds(0, handlers - 1)], key_recv)
 
     plan = []
     for step in range(count + 1):
@@ -394,21 +402,15 @@
     with jax.named_scope("accum"):
         accum_out[...] = state["new"].T[:table_count]
 
-    for d in range(1, handlers):
-        key_copy((me + d) % handlers, me).wait_send()
+    all_in(keys.at[pl.ds(0, handlers - 1)], key_send)
     for slot in range(count):
       with jax.named_scope("sent"):
         wait_sent(slot)
 
         def sent(t):
-            def wait(step, carry):
-                target = (z + 1 + step) % z_count
-                z_copy(slot, target, z).wait_send()
-                return carry
-
-            lax.fori_loop(0, z_count - 1, wait, 0)
-            for d in range(1, handlers):
-                fin_copy(slot, t, (me + d) % handlers, me).wait_send()
+            if z_count > 1:
+                all_in(partial.at[slot, pl.ds(0, z_count - 1)], z_send.at[slot])
+            all_in(fin_out.at[slot, pl.ds(0, handlers - 1)], fin_send.at[slot])
 
         handled(slot, sent)
 
@@ -469,16 +471,9 @@
         pltpu.VMEM((count, handlers, rows_own, width), bf16),
         pltpu.VMEM((table_count, rows_own, width), bf16),
         dma((8,)),
-        dma((count,)),
-        dma((handlers,)),
-        dma((handlers,)),
-        dma((count, handlers)),
-        dma((count, handlers)),
-        dma((count, z_count)),
-        dma((count, z_count)),
-        dma((count, handlers)),
-        dma((count, handlers)),
-    ]
+        dma,
+        dma,
+    ] + [dma((count,)) for _ in range(6)]
     results = pl.pallas_call(
         functools.partial(step_kernel, slots, z_count, mp_count),
         out_shape=tuple(pltpu.VMEM(a.shape, a.dtype) for a in out_shape),

time: 40.9 us -> 39.4 us (0.963)
  Pallas kernels: 40.2 us -> 38.6 us
    pallas_call x1, Pallas kernels: 39.3 us -> 37.8 us  [per_device(): pl.pallas_call(functools.partial(step_kernel, slots, z_count, mp_count),...]
where the time goes in v3:
time: 39.4 us; the launch traced here: 39.2 us
  Pallas kernels  38.6 us (98%)
  between operations  0.64 us (2%)
    pallas_call x1, Pallas kernels, per_device(): pl.pallas_call(functools.partial(step_kernel, slots, z_count, mp_count),...  37.8 us
    pallas_call x1, Pallas kernels, per_device(): pl.pallas_call(emit_kernel, out_shape=out_shape, in_specs=[vmem] * 3, out...  0.81 us

profile of v3, /device:TPU:0, one launch (start us, length us, event | category | flops | bytes accessed | tf_op | source)
XLA Modules:
  0.0 39.2 jit_solution(12462636295966769496)
XLA Ops:
  0.6 37.8 %shard_map.103 = (bf16[256,128]{1,0:T(8,128)(2,1)S(1)}, f32[26,32,128]{2,1,0:T(8,128)S(1)}, f32[26,32]{1,0:T(8,128)S(1)}) custom-call(bf16[26,256,128]{2,1,0:T(8,128)(2,1)} %bitcast.3, bf16[256,128]{1,0:T(8,128)(2,1)} %dense.1, bf16[256,1024]{1,0:T(8,128)(2,1)} %cot.1, bf16[479,1024]{1,0:T(8,128)(2,1)} %weight.1, s32[26,1,256]{2,1,0:T(1,128)} %bitcast.5, ...), custom_call_target="tpu_custom_call" | custom-call | tf_op jit(solution)/shard_map/pallas_call | solution.py:477
  38.4 0.8 %shard_map.104 = (bf16[256,128]{1,0:T(8,128)(2,1)}, f32[26,32,128]{2,1,0:T(8,128)}, f32[26,32]{1,0:T(8,128)}) custom-call(bf16[256,128]{1,0:T(8,128)(2,1)S(1)} %get-tuple-element.6.refs_0_, f32[26,32,128]{2,1,0:T(8,128)S(1)} %get-tuple-element.7.refs_1_, f32[26,32]{1,0:T(8,128)S(1)} %get-tuple-element.8.refs_2_), custom_call_target="tpu_custom_call" | custom-call | tf_op jit(solution)/shard_map/pallas_call | solution.py:490

commit v4 on v3

--- a/solution.py
+++ b/solution.py
@@ -15,35 +15,39 @@
 GROUP = 8
 SPAN = 256
 UNROLL = 4
-PARTS = (2, 14, 26)
+PARTS = (4, 10, 26)
 
 
 def table_slots(table_count, handlers):
     slots = []
     rest = table_count % handlers
-    starts = [0] * (rest > 0) + list(range(rest, table_count, handlers))
-    for start in starts:
-        count = rest if rest and start == 0 else handlers
+    counts = [handlers] * (table_count // handlers)
+    if rest:
+        counts.insert(min(1, len(counts)), rest)
+    start = 0
+    for count in counts:
         if count == handlers:
             slots.append((start, None))
         else:
             step = 2 if 2 * count <= handlers else 1
             owners = [handlers - step * (count - i) for i in range(count)]
             slots.append((start, tuple(owners)))
+        start += count
     return slots
 
 
 def step_kernel(
-    slots, z_count, mp_count,
+    slots, direct, z_count, mp_count,
     sparse, dense, cot, weight, owner, local, table, accum,
     dense_out, table_out, accum_out,
-    feats, cot_v, weight_v, owner_v, local_v, table_v, accum_v,
-    keys, select, repeat, blocks, spread, top, grads, got_rows, got_keys,
-    partial, own_sum, z_in, fin_out, fin_in,
-    load_sem, key_send, key_recv, row_send, row_recv,
-    z_send, z_recv, fin_send, fin_recv,
+    cot_v, weight_v, owner_v, local_v, table_v, accum_v,
+    keys, pair_cot, select, repeat, blocks, spread, top, grads, got_rows, got_keys,
+    partial, own_sum, z_in, fin_out, fin_in, pieces,
+    load_sem, tile_sem, key_send, key_recv, row_send, row_recv,
+    z_send, z_recv, fin_send, fin_recv, direct_send, direct_recv,
 ):
-    table_count, batch_rows, width = sparse.shape
+    table_count, groups, _, width = sparse.shape
+    batch_rows = groups * GROUP
     rows_own = table.shape[1]
     handlers = 2 * mp_count
     rows_grp = rows_own * mp_count
@@ -59,22 +63,41 @@
     def z_device(d):
         return (((z + d) % z_count) * 2 + x, mp)
 
+    def all_in(buffer, sem):
+        pltpu.make_async_copy(buffer, buffer, sem).wait()
+
     loads = [
         pltpu.make_async_copy(source, target, load_sem.at[i])
         for i, (source, target) in enumerate((
             (cot, cot_v), (weight, weight_v), (owner, owner_v), (local, local_v),
-            (sparse, feats.at[pl.ds(0, table_count)]), (dense, feats.at[table_count]),
-            (table, table_v), (accum, accum_v),
+            (dense, blocks.at[:, table_count]), (table, table_v), (accum, accum_v),
         ))
     ]
-    for load in loads:
+    tiles = [
+        pltpu.make_async_copy(
+            sparse.at[:, g], blocks.at[g, pl.ds(0, table_count)],
+            tile_sem.at[g // (2 * UNROLL)],
+        )
+        for g in range(groups)
+    ]
+    for load in loads[:4]:
         load.start()
-
-    peers = [plane_device((me + d) % handlers) for d in range(1, handlers)]
-    peers_z = [z_device(d) for d in range(1, z_count)]
+    blocks[:, pl.ds(feature_count, SPAN // GROUP - feature_count)] = jnp.zeros(
+        (groups, SPAN // GROUP - feature_count, GROUP, width), jnp.bfloat16
+    )
+
     barrier = pltpu.get_barrier_semaphore()
-    for device in peers + peers_z:
-        pl.semaphore_signal(barrier, inc=1, device_id=device, device_id_type=MESH)
+    device_count = 2 * z_count * mp_count
+
+    def greet(step, carry):
+        other = (dp * mp_count + mp + 1 + step) % device_count
+        pl.semaphore_signal(
+            barrier, inc=1, device_id=(other // mp_count, other % mp_count),
+            device_id_type=MESH,
+        )
+        return carry
+
+    lax.fori_loop(0, device_count - 1, greet, 0)
 
     with jax.named_scope("const"):
         pair_count = feature_count * (feature_count - 1) // 2
@@ -95,44 +118,38 @@
         repeat[...] = jnp.where(rep_row == rep_col // GROUP, 1.0, 0.0).astype(jnp.bfloat16)
     with jax.named_scope("loadwait"):
         loads[0].wait()
+        for load in loads[4:5] + tiles + loads[5:]:
+            load.start()
         loads[1].wait()
     input_cot = lax.dot_general(
         cot_v[...], weight_v[...], (((1,), (1,)), ((), ())), preferred_element_type=jnp.float32
     )
     top[...] = input_cot[:, :width]
-    symmetric = jnp.dot(
-        input_cot[:, width:].astype(jnp.bfloat16), select[...], preferred_element_type=jnp.float32
-    ).astype(jnp.bfloat16)
-
-    loads[4].wait()
-    loads[5].wait()
-
-    def build_blocks(i, carry):
-        span = pl.ds(pl.multiple_of(i * 2 * GROUP, 2 * GROUP), 2 * GROUP)
-        both = feats[:, span, :].astype(jnp.float32)
-        pad = jnp.zeros(((feature_pad - feature_count) * GROUP, width), jnp.float32)
-        for half in range(2):
-            part = both[:, half * GROUP : (half + 1) * GROUP, :]
-            part = part.reshape(feature_count * GROUP, width)
-            blocks[2 * i + half] = jnp.concatenate([part, pad], 0).astype(jnp.bfloat16)
-        return carry
+    pair_cot[...] = input_cot[:, width:].astype(jnp.bfloat16)
 
     with jax.named_scope("blocks"):
-        lax.fori_loop(0, batch_rows // (2 * GROUP), build_blocks, 0)
-
+        loads[4].wait()
+
+    features = blocks.reshape(groups, SPAN, width)
     mask = (
         lax.broadcasted_iota(jnp.int32, (GROUP, SPAN), 1) % GROUP
         == lax.broadcasted_iota(jnp.int32, (GROUP, SPAN), 0)
     )
 
     def gradients(first, last):
-        for q in range(first // per_dot, -(-last // per_dot)):
+        for q in range(-(-first // per_dot), -(-last // per_dot)):
+            symmetric = jnp.dot(
+                pair_cot[...], select[:, q * LANES : (q + 1) * LANES],
+                preferred_element_type=jnp.float32,
+            ).astype(jnp.bfloat16)
             spread[:, q * per_dot * SPAN : (q + 1) * per_dot * SPAN] = jnp.dot(
-                symmetric[:, q * LANES : (q + 1) * LANES], repeat[...],
-                preferred_element_type=jnp.float32,
+                symmetric, repeat[...], preferred_element_type=jnp.float32
             )
 
         def one(step, carry):
+            if first == 0:
+                span = pl.ds(step * 2 * UNROLL, 2 * UNROLL)
+                all_in(blocks.at[span, pl.ds(0, table_count)], tile_sem.at[step])
             for i in [step * UNROLL + u for u in range(UNROLL)]:
                 outs = []
                 for half in range(2):
@@ -143,7 +160,7 @@
                     ]
                     lhs = jnp.concatenate(parts, 0).astype(jnp.bfloat16)
                     outs.append(
-                        jnp.dot(lhs, blocks[2 * i + half], preferred_element_type=jnp.float32)
+                        jnp.dot(lhs, features[2 * i + half], preferred_element_type=jnp.float32)
                     )
                 span = pl.ds(pl.multiple_of(i * 2 * GROUP, 2 * GROUP), 2 * GROUP)
                 for t in range(first, last):
@@ -160,9 +177,6 @@
     def table_of(slot, h):
         return slots[slot][0] + h // 2 + (h % 2) * (handlers // 2)
 
-    def all_in(buffer, sem):
-        pltpu.make_async_copy(buffer, buffer, sem).wait()
-
     def row_copy(slot, t, target, source):
         return pltpu.make_async_remote_copy(
             src_ref=grads.at[t],
@@ -268,6 +282,16 @@
             device_id_type=MESH,
         )
 
+    def direct_copy(slot, target, h):
+        return pltpu.make_async_remote_copy(
+            src_ref=partial.at[slot, target, pl.ds(pl.multiple_of(h * rows_own, 16), rows_own)],
+            dst_ref=pieces.at[me * z_count + z],
+            send_sem=direct_send,
+            recv_sem=direct_recv,
+            device_id=(target * 2 + h // mp_count, h % mp_count),
+            device_id_type=MESH,
+        )
+
     def job(slot):
         def body(t):
             with jax.named_scope(f"jobwait{slot}"):
@@ -288,11 +312,22 @@
             def away(step, carry):
                 target = z_order(step)
                 partial[slot, target] = sums(target).astype(jnp.bfloat16)
-                z_copy(slot, target, z).start()
+                if slot == direct:
+                    for h in range(handlers):
+                        direct_copy(slot, target, h).start()
+                else:
+                    z_copy(slot, target, z).start()
                 return carry
 
             lax.fori_loop(0, z_count - 1, away, 0)
-            own_sum[slot] = sums(z)
+            if slot == direct:
+                partial[slot, z] = sums(z).astype(jnp.bfloat16)
+                for d in range(1, handlers):
+                    direct_copy(slot, z, (me + d) % handlers).start()
+                span = pl.ds(pl.multiple_of(me * rows_own, 16), rows_own)
+                pieces[me * z_count + z] = partial[slot, z, span]
+            else:
+                own_sum[slot] = sums(z)
 
         handled(slot, body)
 
@@ -329,7 +364,17 @@
     def update(slot):
         start, owners = slots[slot]
         count = handlers if owners is None else len(owners)
-        if owners is None:
+        span = slice(start, start + count)
+        if slot == direct:
+            all_in(pieces.at[pl.ds(0, handlers * z_count - 1)], direct_recv)
+            parts = [None] * handlers
+            for h in range(handlers):
+                total = pieces[h * z_count].astype(jnp.float32)
+                for source in range(1, z_count):
+                    total = total + pieces[h * z_count + source].astype(jnp.float32)
+                parts[table_of(0, h) - slots[0][0]] = total
+            grad = jnp.stack(parts)
+        elif owners is None:
             all_in(fin_in.at[pl.ds(0, handlers - 1)], fin_recv.at[slot])
         else:
             mine = functools.reduce(jnp.logical_or, [me == h for h in owners])
@@ -340,8 +385,8 @@
                         mine if less else jnp.logical_not(mine),
                         lambda: all_in(fin_in.at[pl.ds(0, came)], fin_recv.at[slot]),
                     )
-        span = slice(start, start + count)
-        grad = fin_in[span].astype(jnp.float32)
+        if slot != direct:
+            grad = fin_in[span].astype(jnp.float32)
         mean = jnp.sum(grad * grad, axis=2, keepdims=True) * (1.0 / width)
         old = jnp.stack([state["old"][:, t : t + 1] for t in range(start, start + count)])
         new = old + mean
@@ -373,15 +418,15 @@
             loads[3].wait()
             build_keys()
             with jax.named_scope("barrier"):
-                pl.semaphore_wait(barrier, handlers - 1 + z_count - 1)
+                pl.semaphore_wait(barrier, device_count - 1)
             send_keys()
         for slot, parity, ready in sends:
             if done < ready <= last or (parity and ready == last == table_count):
                 send_rows(slot, parity)
         done = last
 
+    loads[5].wait()
     loads[6].wait()
-    loads[7].wait()
     old = jnp.concatenate(
         [accum_v[...], jnp.zeros((LANES - table_count, rows_own), jnp.float32)], 0
     )
@@ -393,9 +438,8 @@
     plan = []
     for step in range(count + 1):
         plan += [(job, step)] * (step < count) + [(finish, step - 1)] * (step > 0)
-    last = plan.pop()
-    plan += [(update, slot) for slot in range(count - 2)] + [last]
-    plan += [(update, slot) for slot in range(max(0, count - 2), count)]
+    plan += [(update, slot) for slot in range(count)]
+    plan = [(stage, slot) for stage, slot in plan if stage is not finish or slot != direct]
     for stage, slot in plan:
         with jax.named_scope(f"{stage.__name__}{slot}"):
             stage(slot)
@@ -408,6 +452,9 @@
         wait_sent(slot)
 
         def sent(t):
+            if slot == direct:
+                all_in(pieces.at[pl.ds(0, handlers * z_count - 1)], direct_send)
+                return
             if z_count > 1:
                 all_in(partial.at[slot, pl.ds(0, z_count - 1)], z_send.at[slot])
             all_in(fin_out.at[slot, pl.ds(0, handlers - 1)], fin_send.at[slot])
@@ -430,11 +477,13 @@
 def per_device(sparse_vecs, dense_vec, top_cot, top_weight, owner_ids, local_rows, table, accum):
     batch_rows, table_count, width = sparse_vecs.shape
     rows_own = table.shape[1]
+    groups = batch_rows // GROUP
     z_count = lax.axis_size("dp") // 2
     mp_count = lax.axis_size("mp")
     handlers = 2 * mp_count
     slots = table_slots(table_count, handlers)
     count = len(slots)
+    direct = count - 1 if slots[count - 1][1] is None else None
     block = handlers * rows_own
     feature_count = table_count + 1
     dots = -(-feature_count * (SPAN // GROUP) // LANES)
@@ -449,7 +498,6 @@
         jax.ShapeDtypeStruct(accum.shape, f32),
     )
     scratch = [
-        pltpu.VMEM((feature_count, batch_rows, width), bf16),
         pltpu.VMEM(top_cot.shape, bf16),
         pltpu.VMEM(top_weight.shape, bf16),
         pltpu.VMEM((table_count, 1, batch_rows), i32),
@@ -457,9 +505,10 @@
         pltpu.VMEM(table.shape, f32),
         pltpu.VMEM(accum.shape, f32),
         pltpu.VMEM((handlers, count, 1, batch_rows), i32),
+        pltpu.VMEM((batch_rows, feature_count * table_count // 2), bf16),
         pltpu.VMEM((feature_count * table_count // 2, dots * LANES), bf16),
         pltpu.VMEM((LANES, LANES // (SPAN // GROUP) * SPAN), bf16),
-        pltpu.VMEM((batch_rows // GROUP, SPAN, width), bf16),
+        pltpu.VMEM((groups, SPAN // GROUP, GROUP, width), bf16),
         pltpu.VMEM((batch_rows, dots * (LANES // (SPAN // GROUP)) * SPAN), f32),
         pltpu.VMEM((batch_rows, width), f32),
         pltpu.VMEM((table_count, batch_rows, width), bf16),
@@ -470,12 +519,14 @@
         pltpu.VMEM((count, z_count, block, width), bf16),
         pltpu.VMEM((count, handlers, rows_own, width), bf16),
         pltpu.VMEM((table_count, rows_own, width), bf16),
-        dma((8,)),
+        pltpu.VMEM((handlers * z_count, rows_own, width), bf16),
+        dma((7,)),
+        dma((groups // (2 * UNROLL),)),
         dma,
         dma,
-    ] + [dma((count,)) for _ in range(6)]
+    ] + [dma((count,)) for _ in range(6)] + [dma, dma]
     results = pl.pallas_call(
-        functools.partial(step_kernel, slots, z_count, mp_count),
+        functools.partial(step_kernel, slots, direct, z_count, mp_count),
         out_shape=tuple(pltpu.VMEM(a.shape, a.dtype) for a in out_shape),
         in_specs=[hbm] * 8,
         out_specs=(vmem,) * 3,
@@ -484,7 +535,8 @@
             collective_id=0, has_side_effects=True, vmem_limit_bytes=VMEM_LIMIT
         ),
     )(
-        sparse_vecs.transpose(1, 0, 2), dense_vec, top_cot, top_weight,
+        sparse_vecs.transpose(1, 0, 2).reshape(table_count, groups, GROUP, width),
+        dense_vec.reshape(groups, GROUP, width), top_cot, top_weight,
         owner_ids.transpose(1, 2, 0), local_rows.T, table, accum,
     )
     return pl.pallas_call(

time: 39.4 us -> 38 us (0.964)
  Pallas kernels: 38.6 us -> 37.2 us
    pallas_call x1, Pallas kernels: 37.8 us -> 36.4 us  [per_device(): pl.pallas_call(functools.partial(step_kernel, slots, direct, z_count, mp_...]
where the time goes in v4:
time: 38 us; the launch traced here: 37.9 us
  Pallas kernels  37.2 us (98%)
  between operations  0.64 us (2%)
    pallas_call x1, Pallas kernels, per_device(): pl.pallas_call(functools.partial(step_kernel, slots, direct, z_count, mp_...  36.4 us
    pallas_call x1, Pallas kernels, per_device(): pl.pallas_call(emit_kernel, out_shape=out_shape, in_specs=[vmem] * 3, out...  0.81 us

profile of v4, /device:TPU:0, one launch (start us, length us, event | category | flops | bytes accessed | tf_op | source)
XLA Modules:
  0.0 37.9 jit_solution(10753639463761870323)
XLA Ops:
  0.6 36.4 %shard_map.103 = (bf16[256,128]{1,0:T(8,128)(2,1)S(1)}, f32[26,32,128]{2,1,0:T(8,128)S(1)}, f32[26,32]{1,0:T(8,128)S(1)}) custom-call(bf16[26,32,8,128]{3,2,1,0:T(8,128)(2,1)} %bitcast.6, bf16[32,8,128]{2,1,0:T(8,128)(2,1)} %bitcast.7, bf16[256,1024]{1,0:T(8,128)(2,1)} %cot.1, bf16[479,1024]{1,0:T(8,128)(2,1)} %weight.1, s32[26,1,256]{2,1,0:T(1,128)} %bitcast.9, ...), custom_call_target="tpu_custom_call" | custom-call | tf_op jit(solution)/shard_map/pallas_call | solution.py:528
  37.1 0.8 %shard_map.104 = (bf16[256,128]{1,0:T(8,128)(2,1)}, f32[26,32,128]{2,1,0:T(8,128)}, f32[26,32]{1,0:T(8,128)}) custom-call(bf16[256,128]{1,0:T(8,128)(2,1)S(1)} %get-tuple-element.6.refs_0_, f32[26,32,128]{2,1,0:T(8,128)S(1)} %get-tuple-element.7.refs_1_, f32[26,32]{1,0:T(8,128)S(1)} %get-tuple-element.8.refs_2_), custom_call_target="tpu_custom_call" | custom-call | tf_op jit(solution)/shard_map/pallas_call | solution.py:542

commit v5 on v4

--- a/solution.py
+++ b/solution.py
@@ -14,7 +14,7 @@
 LANES = 128
 GROUP = 8
 SPAN = 256
-UNROLL = 4
+UNROLL = 8
 PARTS = (4, 10, 26)
 
 
@@ -30,7 +30,7 @@
             slots.append((start, None))
         else:
             step = 2 if 2 * count <= handlers else 1
-            owners = [handlers - step * (count - i) for i in range(count)]
+            owners = [i * (handlers - 2) // max(1, count - 1) for i in range(count)]
             slots.append((start, tuple(owners)))
         start += count
     return slots
@@ -203,8 +203,10 @@
     def targets_of(slot, parity):
         start, owners = slots[slot]
         if owners is None:
-            for j in range(1, handlers // 2):
-                h = 2 * ((me // 2 + j) % (handlers // 2)) + parity
+            rows_y = mp_count // 2
+            hops = [(0, j) for j in range(1, rows_y)] + [(1, j) for j in range(rows_y)]
+            for jx, jy in hops:
+                h = 2 * ((x + jx) % 2 * rows_y + (mp // 2 + jy) % rows_y) + parity
                 yield h, table_of(slot, h), None
             h = 2 * (me // 2) + parity
             yield h, table_of(slot, h), me != h

time: 38 us -> 37 us (0.974)
  Pallas kernels: 37.2 us -> 36.2 us
    pallas_call x1, Pallas kernels: 36.4 us -> 35.4 us  [per_device(): pl.pallas_call(functools.partial(step_kernel, slots, direct, z_count, mp_...]
where the time goes in v5:
time: 37 us; the launch traced here: 36.8 us
  Pallas kernels  36.2 us (98%)
  between operations  0.64 us (2%)
    pallas_call x1, Pallas kernels, per_device(): pl.pallas_call(functools.partial(step_kernel, slots, direct, z_count, mp_...  35.4 us
    pallas_call x1, Pallas kernels, per_device(): pl.pallas_call(emit_kernel, out_shape=out_shape, in_specs=[vmem] * 3, out...  0.81 us

profile of v5, /device:TPU:0, one launch (start us, length us, event | category | flops | bytes accessed | tf_op | source)
XLA Modules:
  0.0 36.8 jit_solution(8103187088210231650)
XLA Ops:
  0.6 35.4 %shard_map.103 = (bf16[256,128]{1,0:T(8,128)(2,1)S(1)}, f32[26,32,128]{2,1,0:T(8,128)S(1)}, f32[26,32]{1,0:T(8,128)S(1)}) custom-call(bf16[26,32,8,128]{3,2,1,0:T(8,128)(2,1)} %bitcast.6, bf16[32,8,128]{2,1,0:T(8,128)(2,1)} %bitcast.7, bf16[256,1024]{1,0:T(8,128)(2,1)} %cot.1, bf16[479,1024]{1,0:T(8,128)(2,1)} %weight.1, s32[26,1,256]{2,1,0:T(1,128)} %bitcast.9, ...), custom_call_target="tpu_custom_call" | custom-call | tf_op jit(solution)/shard_map/pallas_call | solution.py:530
  36.0 0.8 %shard_map.104 = (bf16[256,128]{1,0:T(8,128)(2,1)}, f32[26,32,128]{2,1,0:T(8,128)}, f32[26,32]{1,0:T(8,128)}) custom-call(bf16[256,128]{1,0:T(8,128)(2,1)S(1)} %get-tuple-element.6.refs_0_, f32[26,32,128]{2,1,0:T(8,128)S(1)} %get-tuple-element.7.refs_1_, f32[26,32]{1,0:T(8,128)S(1)} %get-tuple-element.8.refs_2_), custom_call_target="tpu_custom_call" | custom-call | tf_op jit(solution)/shard_map/pallas_call | solution.py:544

commit v6 on v5

--- a/solution.py
+++ b/solution.py
@@ -15,7 +15,7 @@
 GROUP = 8
 SPAN = 256
 UNROLL = 8
-PARTS = (4, 10, 26)
+PARTS = (4, 10, 18, 26)
 
 
 def table_slots(table_count, handlers):
@@ -302,13 +302,14 @@
 
             def sums(target):
                 base = target * block
-                total = jnp.zeros((block, width), jnp.float32)
+                total = None
                 for h in range(handlers):
                     onehot = jnp.where(targets == got_keys[h, slot] - base, 1.0, 0.0)
-                    total = total + jnp.dot(
+                    part = jnp.dot(
                         onehot.astype(jnp.bfloat16), got_rows[slot, h],
                         preferred_element_type=jnp.float32,
                     )
+                    total = part if total is None else total + part
                 return total
 
             def away(step, carry):

time: 37 us -> 37 us (level)
  no operation moved by 1% of the time
where the time goes in v6:
time: 37 us; the launch traced here: 36.8 us
  Pallas kernels  36.2 us (98%)
  between operations  0.64 us (2%)
    pallas_call x1, Pallas kernels, per_device(): pl.pallas_call(functools.partial(step_kernel, slots, direct, z_count, mp_...  35.4 us
    pallas_call x1, Pallas kernels, per_device(): pl.pallas_call(emit_kernel, out_shape=out_shape, in_specs=[vmem] * 3, out...  0.81 us

profile of v6, /device:TPU:0, one launch (start us, length us, event | category | flops | bytes accessed | tf_op | source)
XLA Modules:
  0.0 36.8 jit_solution(14997929419312199814)
XLA Ops:
  0.6 35.4 %shard_map.103 = (bf16[256,128]{1,0:T(8,128)(2,1)S(1)}, f32[26,32,128]{2,1,0:T(8,128)S(1)}, f32[26,32]{1,0:T(8,128)S(1)}) custom-call(bf16[26,32,8,128]{3,2,1,0:T(8,128)(2,1)} %bitcast.6, bf16[32,8,128]{2,1,0:T(8,128)(2,1)} %bitcast.7, bf16[256,1024]{1,0:T(8,128)(2,1)} %cot.1, bf16[479,1024]{1,0:T(8,128)(2,1)} %weight.1, s32[26,1,256]{2,1,0:T(1,128)} %bitcast.9, ...), custom_call_target="tpu_custom_call" | custom-call | tf_op jit(solution)/shard_map/pallas_call | solution.py:531
  36.0 0.8 %shard_map.104 = (bf16[256,128]{1,0:T(8,128)(2,1)}, f32[26,32,128]{2,1,0:T(8,128)}, f32[26,32]{1,0:T(8,128)}) custom-call(bf16[256,128]{1,0:T(8,128)(2,1)S(1)} %get-tuple-element.6.refs_0_, f32[26,32,128]{2,1,0:T(8,128)S(1)} %get-tuple-element.7.refs_1_, f32[26,32]{1,0:T(8,128)S(1)} %get-tuple-element.8.refs_2_), custom_call_target="tpu_custom_call" | custom-call | tf_op jit(solution)/shard_map/pallas_call | solution.py:545
